TPU v7x, 32 devices: a whole 2x2x4 slice. The times are simulated.
32 devices in a mesh: south: 4 (over y, x), east: 2 (over core), down: 4 (over z).
Axes of the slice: x: 2, y: 2, z: 4, core: 2. Of those that a mesh axis runs over, the one named last changes fastest.
Arguments:
- field_now: float32 [32, 32, 512, 128], P('south', 'east', 'down'), may hold values from 0.2 to 1.8
- earlier: float32 [32, 32, 512, 128], P('south', 'east', 'down'), may hold values from 0.2 to 1.8
- speed_square: float32 [32, 32, 512, 128], P('south', 'east', 'down'), may hold values from 0.05 to 0.3
Outputs:
- running_total: float32 [32, 32, 512, 128], P('south', 'east', 'down')
- field_now_end: float32 [32, 32, 512, 128], P('south', 'east', 'down')
All inputs are finite; a program needn't handle non-finite values.
Results may differ from a plain program's by a relative error of at most 0.00002.
Values sent between devices are 32-bit elements; how exact they have to be, the bound alone decides.
A program may use at most 320 MiB of HBM per device.

v0:
```python
import functools

import jax
import jax.numpy as jnp
import numpy as np
from jax import lax
from jax.experimental import pallas as pl
from jax.experimental.pallas import tpu as pltpu
from jax.sharding import PartitionSpec as P

STEPS = 4
PIECES = 8
VMEM_LIMIT = 42 * 1024 * 1024
WRITER_LIMIT = 12 * 1024 * 1024
VIA = 1
MESH = pl.DeviceIdType.MESH


def corner_relays(mesh):
    devices = mesh.devices
    if not hasattr(devices.flat[0], "coords"):
        return {}
    south = devices.shape[list(mesh.axis_names).index("south")]
    lines = np.moveaxis(devices, list(mesh.axis_names).index("south"), 0).reshape(south, -1)
    found = {}
    for side, pairs in ((0, [(p, p - 1) for p in range(1, south)]),
                        (1, [(p, p + 1) for p in range(south - 1)])):
        for p, q in pairs:
            choices = set()
            for line in range(lines.shape[1]):
                a, b = lines[p, line].coords, lines[q, line].coords
                differ = [d for d in range(3) if a[d] != b[d]]
                if len(differ) != 2 or any(abs(a[d] - b[d]) != 1 for d in differ):
                    choices.add(None)
                    continue
                corner = list(a)
                corner[differ[VIA]] = b[differ[VIA]]
                at = [r for r in range(south) if list(lines[r, line].coords) == corner]
                choices.add(at[0] if at else None)
            if len(choices) == 1 and None not in choices:
                found[p, side] = choices.pop()
    fits = all(abs(r - (p - 1 if side == 0 else p + 1)) == 1 for (p, side), r in found.items())
    if len(set(found.values())) != len(found) or not fits:
        return {}
    return found


def kernel(
    sizes, relays, u_hbm, e_hbm, c_hbm, c, end, before,
    ab, z, zs, pin, sbuf,
    s_send, s_recv, d_send, d_recv, e_send, e_recv,
    ei_send, ei_recv, di_send, di_recv, p_send, p_recv, load_sem, *hops,
):
    rows, cols, depth, lanes = u_hbm.shape
    pieces = min(PIECES, cols)
    wide = cols // pieces
    place = {axis: lax.axis_index(axis) for axis in sizes}
    below = {axis: place[axis] > 0 for axis in sizes}
    above = {axis: place[axis] < sizes[axis] - 1 for axis in sizes}
    scale = 1.0 / (rows * sizes["south"])

    odd = lax.rem(place["east"], 2) == 1

    def piece(n):
        return jnp.where(odd, n, pieces - 1 - n)

    def target(axis, side):
        step = sizes[axis] - 1 if side == 0 else 1
        return {axis: lax.rem(place[axis] + step, sizes[axis])}

    def sends(axis, side):
        return below[axis] if side == 0 else above[axis]

    def receives(axis, side):
        return above[axis] if side == 0 else below[axis]

    def remote(src, dst, send, recv, axis, side):
        return pltpu.make_async_remote_copy(
            src_ref=src, dst_ref=dst, send_sem=send, recv_sem=recv,
            device_id=target(axis, side), device_id_type=MESH,
        )

    def south(slot, side, n, first=False):
        here = (1, rows)[side]
        there = (rows + 1, 0)[side]
        src = (
            u_hbm.at[here - 1, pl.ds(n * wide, wide)]
            if first else ab.at[slot, here, pl.ds(n * wide + 1, wide)]
        )
        return remote(
            src, ab.at[slot, there, pl.ds(n * wide + 1, wide)],
            s_send.at[slot, side, n], s_recv.at[slot, side, n], "south", side,
        )

    def down(slot, side, n):
        part = (pl.ds(0, 2), pl.ds(n * wide, wide))
        return remote(
            zs.at[(slot, side) + part], z.at[(slot, 1 - side) + part],
            d_send.at[slot, side, n], d_recv.at[slot, side, n], "down", side,
        )

    def down_inner(slot, side):
        part = pl.ds(2, rows - 2)
        return remote(
            zs.at[slot, side, part], z.at[slot, 1 - side, part],
            di_send.at[slot, side], di_recv.at[slot, side], "down", side,
        )

    def east(slot, side, k, first=False):
        here = (1, cols)[side]
        there = (cols + 1, 0)[side]
        row = (1, rows)[k]
        src = u_hbm.at[row - 1, here - 1] if first else ab.at[slot, row, here]
        return remote(
            src, ab.at[slot, row, there],
            e_send.at[slot, side, k], e_recv.at[slot, side, k], "east", side,
        )

    def east_inner(slot, side, first=False):
        here = (1, cols)[side]
        there = (cols + 1, 0)[side]
        src = (
            u_hbm.at[pl.ds(1, rows - 2), here - 1]
            if first else ab.at[slot, pl.ds(2, rows - 2), here]
        )
        return remote(
            src, ab.at[slot, pl.ds(2, rows - 2), there],
            ei_send.at[slot, side], ei_recv.at[slot, side], "east", side,
        )

    square = False
    if relays:
        relay_buf, h_recv, h_send, held, q_send, q_recv = hops
    square = sizes["south"] == 4 and relays == {(2, 0): 0, (1, 1): 3}

    def by_place(table, other):
        value = jnp.int32(other)
        for p, entry in table.items():
            value = jnp.where(place["south"] == p, entry, value)
        return value

    relay_at = [
        by_place({p: r for (p, s), r in relays.items() if s == side}, -1) for side in (0, 1)
    ]
    served = by_place({r: p for (p, _), r in relays.items()}, -1)
    served_side = by_place({r: side for (_, side), r in relays.items()}, 0)
    is_relay = served >= 0

    def hop_in(t, slot, side, n, m, first=False):
        here = (1, rows)[side]
        src = (
            u_hbm.at[here - 1, pl.ds(n * wide, wide)]
            if first else ab.at[slot, here, pl.ds(n * wide + 1, wide)]
        )
        return pltpu.make_async_remote_copy(
            src_ref=src, dst_ref=relay_buf.at[t, m],
            send_sem=s_send.at[slot, side, n], recv_sem=h_recv.at[t, m],
            device_id={"south": jnp.maximum(relay_at[side], 0)}, device_id_type=MESH,
        )

    def hop_out(t, m):
        n = piece(2 * m + 1)
        slot = lax.rem(jnp.int32(t), 2)
        there = jnp.where(served_side == 0, rows + 1, 0)
        goal = served + 2 * served_side - 1
        return pltpu.make_async_remote_copy(
            src_ref=relay_buf.at[t, m],
            dst_ref=ab.at[slot, there, pl.ds(n * wide + 1, wide)],
            send_sem=h_send.at[t, m], recv_sem=s_recv.at[slot, served_side, n],
            device_id={"south": jnp.maximum(goal, 0)}, device_id_type=MESH,
        )

    def forward(t, m):
        if relays:
            @pl.when(is_relay)
            def _():
                hop_in(t, 0, 0, 0, m).wait_recv()
                hop_out(t, m).start()

    def send_south(t, slot, turn, first=False):
        n = piece(turn)
        for side in (0, 1):
            here = sends("south", side)
            if relays:
                bent = jnp.logical_and(relay_at[side] >= 0, lax.rem(turn, 2) == 1)

                @pl.when(jnp.logical_and(here, bent))
                def _():
                    hop_in(t, slot, side, n, turn // 2, first).start()

                here = jnp.logical_and(here, jnp.logical_not(bent))

            @pl.when(here)
            def _():
                south(slot, side, n, first).start()

    def each(act, when, axis, copy):
        for side in (0, 1):
            @pl.when(when(axis, side))
            def _():
                getattr(copy(side), act)()

    barrier = pltpu.get_barrier_semaphore()
    for axis in sizes:
        for side in (0, 1):
            @pl.when(sends(axis, side))
            def _():
                pl.semaphore_signal(
                    barrier, inc=1, device_id=target(axis, side), device_id_type=MESH
                )
    met = 0
    if relays:
        for side in (0, 1):
            @pl.when(relay_at[side] >= 0)
            def _():
                pl.semaphore_signal(
                    barrier, inc=1, device_id={"south": jnp.maximum(relay_at[side], 0)},
                    device_id_type=MESH,
                )

            met = met + (relay_at[side] >= 0).astype(jnp.int32)

        @pl.when(is_relay)
        def _():
            pl.semaphore_signal(
                barrier, inc=1, device_id={"south": jnp.maximum(served, 0)},
                device_id_type=MESH,
            )

        met = met + is_relay.astype(jnp.int32)
    for axis in sizes:
        met = met + below[axis].astype(jnp.int32) + above[axis].astype(jnp.int32)

    own = (pl.ds(1, rows), pl.ds(1, cols))
    loads = [
        pltpu.make_async_copy(u_hbm, ab.at[(0,) + own], load_sem.at[0]),
        pltpu.make_async_copy(e_hbm, ab.at[(1,) + own], load_sem.at[1]),
        pltpu.make_async_copy(c_hbm, c, load_sem.at[2]),
    ]
    loads[0].start()
    pl.semaphore_wait(barrier, met)

    @pl.loop(0, pieces)
    def _(n):
        send_south(0, 0, n, True)

    for k in (0, 1):
        each("start", sends, "east", lambda side: east(0, side, k, True))
    each("start", sends, "east", lambda side: east_inner(0, side, True))
    loads[1].start()
    loads[2].start()

    blank = jnp.zeros((depth, lanes), jnp.float32)
    for side, missing in ((0, below), (1, above)):
        @pl.when(jnp.logical_not(missing["south"]))
        def _():
            @pl.loop(0, cols)
            def _(i):
                for slot in (0, 1):
                    ab[slot, (0, rows + 1)[side], i + 1] = blank

        @pl.when(jnp.logical_not(missing["east"]))
        def _():
            @pl.loop(0, rows)
            def _(j):
                for slot in (0, 1):
                    ab[slot, j + 1, (0, cols + 1)[side]] = blank

        @pl.when(jnp.logical_not(missing["down"]))
        def _():
            @pl.loop(0, cols)
            def _(i):
                for slot in (0, 1):
                    for r in range(rows):
                        z[slot, side, r, i] = blank[:1]

    loads[0].wait()

    @pl.loop(0, cols)
    def _(i):
        for r in range(rows):
            j = 0 if r == 0 else rows - 1 if r == 1 else r - 1
            zs[0, 0, r, i] = ab[0, j + 1, i + 1, pl.ds(0, 1)]
            zs[0, 1, r, i] = ab[0, j + 1, i + 1, pl.ds(depth - 1, 1)]

    @pl.loop(0, pieces)
    def _(n):
        each("start", sends, "down", lambda side: down(0, side, piece(n)))

    each("start", sends, "down", lambda side: down_inner(0, side))
    loads[1].wait()
    loads[2].wait()

    for m in range(pieces // 2):
        forward(0, m)

    level = lax.broadcasted_iota(jnp.int32, (depth, lanes), 0)

    def cell(now, later, j, i, r, final=False):
        x = ab[now, j + 1, i + 1]
        lower = jnp.where(level == 0, z[now, 0, r, i], pltpu.roll(x, 1, 0))
        upper = jnp.where(level == depth - 1, z[now, 1, r, i], pltpu.roll(x, depth - 1, 0))
        spread = (
            ab[now, j, i + 1] + ab[now, j + 2, i + 1]
            + ab[now, j + 1, i] + ab[now, j + 1, i + 2]
            + lower + upper - 6.0 * x
        )
        new = 2.0 * x - ab[later, j + 1, i + 1] + c[j, i] * spread
        if final:
            end[j, i] = new
            return
        ab[later, j + 1, i + 1] = new
        zs[later, 0, r, i] = new[:1]
        zs[later, 1, r, i] = new[depth - 1:]

    def inner(step, now, later, final=False):
        each("wait_recv", receives, "east", lambda side: east_inner(now, side))
        each("wait_recv", receives, "down", lambda side: down_inner(now, side))

        @pl.when(step >= 1)
        def _():
            each("wait_send", sends, "east", lambda side: east_inner(later, side))
            each("wait_send", sends, "down", lambda side: down_inner(later, side))

        @pl.loop(1, rows - 1)
        def _(j):
            @pl.loop(0, cols)
            def _(i):
                cell(now, later, j, i, j + 1, final)

        @pl.when(step < STEPS - 1)
        def _():
            each("start", sends, "east", lambda side: east_inner(later, side))
            each("start", sends, "down", lambda side: down_inner(later, side))

    def outer_edges(act, when, slot, n):
        for side in (0, 1):
            end = (0, pieces - 1)[side if when is sends else 1 - side]

            @pl.when(jnp.logical_and(when("east", side), n == end))
            def _():
                for k in (0, 1):
                    getattr(east(slot, side, k), act)()

    def outer_piece(step, now, later, turn, final=False):
        n = piece(turn)
        each("wait_recv", receives, "south", lambda side: south(now, side, n))
        each("wait_recv", receives, "down", lambda side: down(now, side, n))
        outer_edges("wait_recv", receives, now, n)

        @pl.when(step >= 1)
        def _():
            each("wait_send", sends, "south", lambda side: south(later, side, n))
            each("wait_send", sends, "down", lambda side: down(later, side, n))
            outer_edges("wait_send", sends, later, n)

        @pl.loop(0, wide)
        def _(w):
            i = n * wide + w
            cell(now, later, 0, i, 0, final)
            cell(now, later, rows - 1, i, 1, final)

        @pl.when(step < STEPS - 1)
        def _():
            send_south(step + 1, later, turn)
            each("start", sends, "down", lambda side: down(later, side, n))
            outer_edges("start", sends, later, n)

    @pl.loop(0, STEPS - 1)
    def _(step):
        now = lax.rem(step, 2)
        inner(step, now, 1 - now)

        @pl.loop(0, pieces)
        def _(n):
            outer_piece(step, now, 1 - now, n)
            if relays:
                @pl.when(jnp.logical_and(lax.rem(n, 2) == 1, n >= 3))
                def _():
                    forward(step + 1, n // 2 - 1)

        if relays:
            forward(step + 1, pieces // 2 - 1)

    last = STEPS - 1
    now, later = last % 2, 1 - last % 2
    inner(last, now, later, True)

    def carry(n):
        return remote(
            sbuf.at[pl.ds(n * wide, wide)], pin.at[pl.ds(n * wide, wide)],
            p_send.at[n], p_recv.at[n], "south", 1,
        )

    first = jnp.logical_not(below["south"])
    spot = place["south"]

    def total_copy(n, src, dst, way, kind, goal):
        part = pl.ds(n * wide, wide)
        return pltpu.make_async_remote_copy(
            src_ref=src.at[part], dst_ref=dst.at[part],
            send_sem=q_send.at[way, n], recv_sem=q_recv.at[kind, n],
            device_id={"south": goal}, device_id_type=MESH,
        )

    def beside(n):
        return total_copy(n, sbuf, pin, 0, 0, lax.rem(spot + 1, 4))

    def across(n):
        return total_copy(n, sbuf, pin, 1, 0, 2)

    def upward(n):
        return total_copy(n, sbuf, held, 1, 1, 3)

    def onward(n):
        return total_copy(n, held, held, 1, 1, 2)

    def middle_total(turn):
        n = piece(turn)

        @pl.when(spot == 2)
        def _():
            beside(n).wait_recv()

            @pl.loop(0, wide)
            def _(w):
                i = n * wide + w
                sbuf[i] = pin[i] + c[rows - 1, i]

            beside(n).start()

        @pl.when(spot == 3)
        def _():
            upward(n).wait_recv()
            onward(n).start()

    @pl.loop(0, pieces)
    def _(turn):
        n = piece(turn)
        outer_piece(last, now, later, turn, True)

        @pl.loop(0, wide)
        def _(w):
            i = n * wide + w
            sum_here = jnp.zeros((depth, lanes), jnp.float32)
            for j in range(rows):
                sum_here = sum_here + end[j, i]
                c[j, i] = sum_here * scale

        if square:
            @pl.when(spot < 2)
            def _():
                @pl.loop(0, wide)
                def _(w):
                    i = n * wide + w
                    sbuf[i] = c[rows - 1, i]

            @pl.when(spot == 0)
            def _():
                beside(n).start()
                across(n).start()

            @pl.when(spot == 1)
            def _():
                upward(n).start()

            @pl.when(turn >= 2)
            def _():
                middle_total(turn - 2)
        else:
            @pl.when(first)
            def _():
                @pl.loop(0, wide)
                def _(w):
                    i = n * wide + w
                    sbuf[i] = c[rows - 1, i]

                @pl.when(above["south"])
                def _():
                    carry(n).start()

    @pl.when(first)
    def _():
        @pl.loop(0, cols)
        def _(i):
            before[i] = blank

    if square:
        @pl.loop(pieces - 2, pieces)
        def _(turn):
            middle_total(turn)

        @pl.when(spot == 1)
        def _():
            @pl.loop(0, pieces)
            def _(turn):
                n = piece(turn)
                beside(n).wait_recv()

                @pl.loop(0, wide)
                def _(w):
                    i = n * wide + w
                    before[i] = pin[i]

        @pl.when(spot >= 2)
        def _():
            @pl.loop(0, pieces)
            def _(turn):
                n = piece(turn)

                @pl.when(spot == 2)
                def _():
                    upward(n).wait_recv()

                @pl.when(spot == 3)
                def _():
                    beside(n).wait_recv()

                @pl.loop(0, wide)
                def _(w):
                    i = n * wide + w
                    before[i] = pin[i] + held[i]
    else:
        @pl.when(below["south"])
        def _():
            @pl.loop(0, pieces)
            def _(turn):
                n = piece(turn)
                carry(n).wait_recv()

                @pl.loop(0, wide)
                def _(w):
                    i = n * wide + w
                    sbuf[i] = c[rows - 1, i] + pin[i]
                    before[i] = pin[i]

                @pl.when(above["south"])
                def _():
                    carry(n).start()

    if relays:
        @pl.when(is_relay)
        def _():
            for t in range(STEPS):
                for m in range(pieces // 2):
                    hop_out(t, m).wait_send()

    each("wait_send", sends, "east", lambda side: east_inner(now, side))
    each("wait_send", sends, "down", lambda side: down_inner(now, side))
    for k in (0, 1):
        each("wait_send", sends, "east", lambda side: east(now, side, k))

    @pl.loop(0, pieces)
    def _(n):
        each("wait_send", sends, "south", lambda side: south(now, side, n))
        each("wait_send", sends, "down", lambda side: down(now, side, n))

        if square:
            @pl.when(lax.rem(spot, 2) == 0)
            def _():
                beside(n).wait_send()

            @pl.when(spot != 2)
            def _():
                across(n).wait_send()
        else:
            @pl.when(above["south"])
            def _():
                carry(n).wait_send()


def writer(part, end, before, total_hbm, end_hbm, total, t_sem, e_sem):
    rows, cols = part.shape[:2]
    ends = [pltpu.make_async_copy(end.at[j], end_hbm.at[j], e_sem.at[j]) for j in range(rows)]
    totals = [
        pltpu.make_async_copy(total.at[j], total_hbm.at[j], t_sem.at[j]) for j in range(rows)
    ]
    for copy in ends:
        copy.start()
    for j in range(rows):
        @pl.loop(0, cols)
        def _(i):
            total[j, i] = part[j, i] + before[i]

        totals[j].start()
    for copy in ends + totals:
        copy.wait()


def shards(sizes, relays, field_now, earlier, speed_square):
    rows, cols, depth, lanes = field_now.shape
    pieces = min(PIECES, cols)
    relays = relays if pieces % 2 == 0 else {}
    edge = (2, 2, rows, cols, 1, lanes)
    dma = pltpu.SemaphoreType.DMA
    anywhere = pl.BlockSpec(memory_space=pltpu.HBM)
    inside = pl.BlockSpec(memory_space=pltpu.VMEM)
    part, end, before = pl.pallas_call(
        functools.partial(kernel, sizes, relays),
        out_shape=(
            pltpu.VMEM(field_now.shape, jnp.float32),
            pltpu.VMEM(field_now.shape, jnp.float32),
            pltpu.VMEM((cols, depth, lanes), jnp.float32),
        ),
        in_specs=[anywhere] * 3,
        out_specs=(inside,) * 3,
        scratch_shapes=[
            pltpu.VMEM((2, rows + 2, cols + 2, depth, lanes), jnp.float32),
            pltpu.VMEM(edge, jnp.float32),
            pltpu.VMEM(edge, jnp.float32),
            pltpu.VMEM((cols, depth, lanes), jnp.float32),
            pltpu.VMEM((cols, depth, lanes), jnp.float32),
            dma((2, 2, pieces)), dma((2, 2, pieces)),
            dma((2, 2, pieces)), dma((2, 2, pieces)),
            dma((2, 2, 2)), dma((2, 2, 2)),
            dma((2, 2)), dma((2, 2)), dma((2, 2)), dma((2, 2)),
            dma((pieces,)), dma((pieces,)), dma((3,)),
        ] + ([
            pltpu.VMEM((STEPS, pieces // 2, cols // pieces, depth, lanes), jnp.float32),
            dma((STEPS, pieces // 2)), dma((STEPS, pieces // 2)),
            pltpu.VMEM((cols, depth, lanes), jnp.float32),
            dma((2, pieces)), dma((2, pieces)),
        ] if relays else []),
        compiler_params=pltpu.CompilerParams(
            collective_id=0, has_side_effects=True, vmem_limit_bytes=VMEM_LIMIT
        ),
        name="wave",
    )(field_now, earlier, speed_square)
    return pl.pallas_call(
        writer,
        out_shape=(jax.ShapeDtypeStruct(field_now.shape, jnp.float32),) * 2,
        in_specs=[inside] * 3,
        out_specs=(anywhere,) * 2,
        scratch_shapes=[pltpu.VMEM(field_now.shape, jnp.float32), dma((rows,)), dma((rows,))],
        compiler_params=pltpu.CompilerParams(vmem_limit_bytes=WRITER_LIMIT),
        name="write",
    )(part, end, before)


def solution(mesh):
    placed = P("south", "east", "down", None)
    sizes = {axis: mesh.shape[axis] for axis in ("south", "east", "down")}
    relays = corner_relays(mesh)
    return jax.shard_map(
        functools.partial(shards, sizes, relays),
        mesh=mesh,
        in_specs=(placed,) * 3,
        out_specs=(placed,) * 2,
        check_vma=False,
    )
```

profile of v0, /device:TPU:4, one launch (start us, length us, event | category | flops | bytes accessed | tf_op | source)
XLA Modules:
  0.0 170.0 jit_solution(10512329750971285121)
XLA Ops:
  0.6 163.4 %wave.1 = (f32[8,16,128,128]{3,2,1,0:T(8,128)S(1)}, f32[8,16,128,128]{3,2,1,0:T(8,128)S(1)}, f32[16,128,128]{2,1,0:T(8,128)S(1)}) custom-call(f32[8,16,128,128]{3,2,1,0:T(8,128)} %u_hbm.1, f32[8,16,128,128]{3,2,1,0:T(8,128)} %e_hbm.1, f32[8,16,128,128]{3,2,1,0:T(8,128)} %c_hbm.1), custom_call_target="tpu_custom_call" | custom-call | tf_op jit(solution)/shard_map/wave/pallas_call | solution.py:598
  164.1 6.0 %write.1 = (f32[8,16,128,128]{3,2,1,0:T(8,128)}, f32[8,16,128,128]{3,2,1,0:T(8,128)}) custom-call(f32[8,16,128,128]{3,2,1,0:T(8,128)S(1)} %get-tuple-element.5.part, f32[8,16,128,128]{3,2,1,0:T(8,128)S(1)} %get-tuple-element.6.end, f32[16,128,128]{2,1,0:T(8,128)S(1)} %get-tuple-element.7.before), custom_call_target="tpu_custom_call" | custom-call | tf_op jit(solution)/shard_map/write/pallas_call | solution.py:629
where the time goes:
time: 170 us
  Pallas kernels  169 us (99%)
    pallas_call x1, Pallas kernels, shards(): pl.pallas_call(functools.partial(kernel, sizes, relays), out_shape=(pltpu...  163 us
    pallas_call x1, Pallas kernels, shards(): pl.pallas_call(writer, out_shape=(jax.ShapeDtypeStruct(field_now.shape, j...  5.96 us

commit v1 on v0

--- a/solution.py
+++ b/solution.py
@@ -80,15 +80,12 @@
             device_id=target(axis, side), device_id_type=MESH,
         )
 
-    def south(slot, side, n, first=False):
+    def south(slot, side, n):
         here = (1, rows)[side]
         there = (rows + 1, 0)[side]
-        src = (
-            u_hbm.at[here - 1, pl.ds(n * wide, wide)]
-            if first else ab.at[slot, here, pl.ds(n * wide + 1, wide)]
-        )
         return remote(
-            src, ab.at[slot, there, pl.ds(n * wide + 1, wide)],
+            ab.at[slot, here, pl.ds(n * wide + 1, wide)],
+            ab.at[slot, there, pl.ds(n * wide + 1, wide)],
             s_send.at[slot, side, n], s_recv.at[slot, side, n], "south", side,
         )
 
@@ -146,14 +143,11 @@
     served_side = by_place({r: side for (_, side), r in relays.items()}, 0)
     is_relay = served >= 0
 
-    def hop_in(t, slot, side, n, m, first=False):
+    def hop_in(t, slot, side, n, m):
         here = (1, rows)[side]
-        src = (
-            u_hbm.at[here - 1, pl.ds(n * wide, wide)]
-            if first else ab.at[slot, here, pl.ds(n * wide + 1, wide)]
-        )
         return pltpu.make_async_remote_copy(
-            src_ref=src, dst_ref=relay_buf.at[t, m],
+            src_ref=ab.at[slot, here, pl.ds(n * wide + 1, wide)],
+            dst_ref=relay_buf.at[t, m],
             send_sem=s_send.at[slot, side, n], recv_sem=h_recv.at[t, m],
             device_id={"south": jnp.maximum(relay_at[side], 0)}, device_id_type=MESH,
         )
@@ -177,7 +171,7 @@
                 hop_in(t, 0, 0, 0, m).wait_recv()
                 hop_out(t, m).start()
 
-    def send_south(t, slot, turn, first=False):
+    def send_south(t, slot, turn):
         n = piece(turn)
         for side in (0, 1):
             here = sends("south", side)
@@ -186,19 +180,36 @@
 
                 @pl.when(jnp.logical_and(here, bent))
                 def _():
-                    hop_in(t, slot, side, n, turn // 2, first).start()
+                    hop_in(t, slot, side, n, turn // 2).start()
 
                 here = jnp.logical_and(here, jnp.logical_not(bent))
 
             @pl.when(here)
             def _():
-                south(slot, side, n, first).start()
+                south(slot, side, n).start()
 
     def each(act, when, axis, copy):
         for side in (0, 1):
             @pl.when(when(axis, side))
             def _():
                 getattr(copy(side), act)()
+
+    def row_load(first, count, sem):
+        return pltpu.make_async_copy(
+            u_hbm.at[pl.ds(first, count)],
+            ab.at[0, pl.ds(first + 1, count), pl.ds(1, cols)], load_sem.at[sem],
+        )
+
+    edge_loads = [row_load(0, 1, 3), row_load(rows - 1, 1, 4)]
+    loads = [
+        row_load(1, rows - 2, 0),
+        pltpu.make_async_copy(
+            e_hbm, ab.at[1, pl.ds(1, rows), pl.ds(1, cols)], load_sem.at[1]
+        ),
+        pltpu.make_async_copy(c_hbm, c, load_sem.at[2]),
+    ]
+    for copy in edge_loads + loads[:1]:
+        copy.start()
 
     barrier = pltpu.get_barrier_semaphore()
     for axis in sizes:
@@ -231,18 +242,13 @@
     for axis in sizes:
         met = met + below[axis].astype(jnp.int32) + above[axis].astype(jnp.int32)
 
-    own = (pl.ds(1, rows), pl.ds(1, cols))
-    loads = [
-        pltpu.make_async_copy(u_hbm, ab.at[(0,) + own], load_sem.at[0]),
-        pltpu.make_async_copy(e_hbm, ab.at[(1,) + own], load_sem.at[1]),
-        pltpu.make_async_copy(c_hbm, c, load_sem.at[2]),
-    ]
-    loads[0].start()
     pl.semaphore_wait(barrier, met)
+    for copy in edge_loads:
+        copy.wait()
 
     @pl.loop(0, pieces)
     def _(n):
-        send_south(0, 0, n, True)
+        send_south(0, 0, n)
 
     for k in (0, 1):
         each("start", sends, "east", lambda side: east(0, side, k, True))
@@ -614,7 +620,7 @@
             dma((2, 2, pieces)), dma((2, 2, pieces)),
             dma((2, 2, 2)), dma((2, 2, 2)),
             dma((2, 2)), dma((2, 2)), dma((2, 2)), dma((2, 2)),
-            dma((pieces,)), dma((pieces,)), dma((3,)),
+            dma((pieces,)), dma((pieces,)), dma((5,)),
         ] + ([
             pltpu.VMEM((STEPS, pieces // 2, cols // pieces, depth, lanes), jnp.float32),
             dma((STEPS, pieces // 2)), dma((STEPS, pieces // 2)),

time: 170 us -> 170 us (level)
  no operation moved by 1% of the time
where the time goes in v1:
time: 170 us
  Pallas kernels  169 us (99%)
    pallas_call x1, Pallas kernels, shards(): pl.pallas_call(functools.partial(kernel, sizes, relays), out_shape=(pltpu...  163 us
    pallas_call x1, Pallas kernels, shards(): pl.pallas_call(writer, out_shape=(jax.ShapeDtypeStruct(field_now.shape, j...  5.96 us

profile of v1, /device:TPU:4, one launch (start us, length us, event | category | flops | bytes accessed | tf_op | source)
XLA Modules:
  0.0 170.0 jit_solution(4298876880681872655)
XLA Ops:
  0.6 163.4 %wave.1 = (f32[8,16,128,128]{3,2,1,0:T(8,128)S(1)}, f32[8,16,128,128]{3,2,1,0:T(8,128)S(1)}, f32[16,128,128]{2,1,0:T(8,128)S(1)}) custom-call(f32[8,16,128,128]{3,2,1,0:T(8,128)} %u_hbm.1, f32[8,16,128,128]{3,2,1,0:T(8,128)} %e_hbm.1, f32[8,16,128,128]{3,2,1,0:T(8,128)} %c_hbm.1), custom_call_target="tpu_custom_call" | custom-call | tf_op jit(solution)/shard_map/wave/pallas_call | solution.py:604
  164.1 6.0 %write.1 = (f32[8,16,128,128]{3,2,1,0:T(8,128)}, f32[8,16,128,128]{3,2,1,0:T(8,128)}) custom-call(f32[8,16,128,128]{3,2,1,0:T(8,128)S(1)} %get-tuple-element.5.part, f32[8,16,128,128]{3,2,1,0:T(8,128)S(1)} %get-tuple-element.6.end, f32[16,128,128]{2,1,0:T(8,128)S(1)} %get-tuple-element.7.before), custom_call_target="tpu_custom_call" | custom-call | tf_op jit(solution)/shard_map/write/pallas_call | solution.py:635

commit v2 on v0

--- a/solution.py
+++ b/solution.py
@@ -412,6 +412,9 @@
     def upward(n):
         return total_copy(n, sbuf, held, 1, 1, 3)
 
+    def direct(n):
+        return total_copy(n, sbuf, held, 0, 1, 2)
+
     def onward(n):
         return total_copy(n, held, held, 1, 1, 2)
 
@@ -432,7 +435,10 @@
         @pl.when(spot == 3)
         def _():
             upward(n).wait_recv()
-            onward(n).start()
+
+            @pl.when(lax.rem(turn, 2) == 1)
+            def _():
+                onward(n).start()
 
     @pl.loop(0, pieces)
     def _(turn):
@@ -464,6 +470,10 @@
             def _():
                 upward(n).start()
 
+                @pl.when(lax.rem(turn, 2) == 0)
+                def _():
+                    direct(n).start()
+
             @pl.when(turn >= 2)
             def _():
                 middle_total(turn - 2)
@@ -490,6 +500,24 @@
         def _(turn):
             middle_total(turn)
 
+    if relays:
+        @pl.when(is_relay)
+        def _():
+            for t in range(STEPS):
+                for m in range(pieces // 2):
+                    hop_out(t, m).wait_send()
+
+    each("wait_send", sends, "east", lambda side: east_inner(now, side))
+    each("wait_send", sends, "down", lambda side: down_inner(now, side))
+    for k in (0, 1):
+        each("wait_send", sends, "east", lambda side: east(now, side, k))
+
+    @pl.loop(0, pieces)
+    def _(n):
+        each("wait_send", sends, "south", lambda side: south(now, side, n))
+        each("wait_send", sends, "down", lambda side: down(now, side, n))
+
+    if square:
         @pl.when(spot == 1)
         def _():
             @pl.loop(0, pieces)
@@ -538,29 +566,17 @@
                 def _():
                     carry(n).start()
 
-    if relays:
-        @pl.when(is_relay)
-        def _():
-            for t in range(STEPS):
-                for m in range(pieces // 2):
-                    hop_out(t, m).wait_send()
-
-    each("wait_send", sends, "east", lambda side: east_inner(now, side))
-    each("wait_send", sends, "down", lambda side: down_inner(now, side))
-    for k in (0, 1):
-        each("wait_send", sends, "east", lambda side: east(now, side, k))
-
     @pl.loop(0, pieces)
-    def _(n):
-        each("wait_send", sends, "south", lambda side: south(now, side, n))
-        each("wait_send", sends, "down", lambda side: down(now, side, n))
+    def _(turn):
+        n = piece(turn)
+        half = lax.rem(turn, 2)
 
         if square:
-            @pl.when(lax.rem(spot, 2) == 0)
+            @pl.when(jnp.logical_or(lax.rem(spot, 2) == 0, jnp.logical_and(spot == 1, half == 0)))
             def _():
                 beside(n).wait_send()
 
-            @pl.when(spot != 2)
+            @pl.when(jnp.logical_or(spot < 2, jnp.logical_and(spot == 3, half == 1)))
             def _():
                 across(n).wait_send()
         else:

time: 170 us -> 170 us (level)
  no operation moved by 1% of the time
where the time goes in v2:
time: 170 us; the launch traced here: 169 us
  Pallas kernels  169 us (99%)
    pallas_call x1, Pallas kernels, shards(): pl.pallas_call(functools.partial(kernel, sizes, relays), out_shape=(pltpu...  163 us
    pallas_call x1, Pallas kernels, shards(): pl.pallas_call(writer, out_shape=(jax.ShapeDtypeStruct(field_now.shape, j...  5.96 us

profile of v2, /device:TPU:4, one launch (start us, length us, event | category | flops | bytes accessed | tf_op | source)
XLA Modules:
  0.0 169.2 jit_solution(17354659068340176329)
XLA Ops:
  0.6 162.6 %wave.1 = (f32[8,16,128,128]{3,2,1,0:T(8,128)S(1)}, f32[8,16,128,128]{3,2,1,0:T(8,128)S(1)}, f32[16,128,128]{2,1,0:T(8,128)S(1)}) custom-call(f32[8,16,128,128]{3,2,1,0:T(8,128)} %u_hbm.1, f32[8,16,128,128]{3,2,1,0:T(8,128)} %e_hbm.1, f32[8,16,128,128]{3,2,1,0:T(8,128)} %c_hbm.1), custom_call_target="tpu_custom_call" | custom-call | tf_op jit(solution)/shard_map/wave/pallas_call | solution.py:614
  163.2 6.0 %write.1 = (f32[8,16,128,128]{3,2,1,0:T(8,128)}, f32[8,16,128,128]{3,2,1,0:T(8,128)}) custom-call(f32[8,16,128,128]{3,2,1,0:T(8,128)S(1)} %get-tuple-element.5.part, f32[8,16,128,128]{3,2,1,0:T(8,128)S(1)} %get-tuple-element.6.end, f32[16,128,128]{2,1,0:T(8,128)S(1)} %get-tuple-element.7.before), custom_call_target="tpu_custom_call" | custom-call | tf_op jit(solution)/shard_map/write/pallas_call | solution.py:645

commit v3 on v0

--- a/solution.py
+++ b/solution.py
@@ -48,12 +48,22 @@
 def kernel(
     sizes, relays, u_hbm, e_hbm, c_hbm, c, end, before,
     ab, z, zs, pin, sbuf,
-    s_send, s_recv, d_send, d_recv, e_send, e_recv,
-    ei_send, ei_recv, di_send, di_recv, p_send, p_recv, load_sem, *hops,
+    s_send, s_recv, d_send, d_recv, e_send, e_recv, ei_recv, di_recv, load_sem, *extra,
 ):
     rows, cols, depth, lanes = u_hbm.shape
     pieces = min(PIECES, cols)
     wide = cols // pieces
+    groups = d_recv.shape[2]
+    turns = pieces // groups
+    square = is_square(sizes, relays)
+    extra = list(extra)
+    if relays:
+        relay_buf, h_recv, h_send = extra[:3]
+        del extra[:3]
+    if square:
+        held, q_send, q_recv = extra
+    else:
+        p_send, p_recv = extra
     place = {axis: lax.axis_index(axis) for axis in sizes}
     below = {axis: place[axis] > 0 for axis in sizes}
     above = {axis: place[axis] < sizes[axis] - 1 for axis in sizes}
@@ -89,21 +99,34 @@
         )
         return remote(
             src, ab.at[slot, there, pl.ds(n * wide + 1, wide)],
-            s_send.at[slot, side, n], s_recv.at[slot, side, n], "south", side,
-        )
-
-    def down(slot, side, n):
-        part = (pl.ds(0, 2), pl.ds(n * wide, wide))
+            s_send.at[slot, side], s_recv.at[slot, side, n], "south", side,
+        )
+
+    def south_sent(slot, side):
+        row = ab.at[slot, (1, rows)[side], pl.ds(1, cols)]
+        return remote(
+            row, row, s_send.at[slot, side], s_recv.at[slot, side, 0], "south", side
+        )
+
+    def down(slot, side, group):
+        start = jnp.where(odd, group, groups - 1 - group) * turns * wide
+        part = (pl.ds(0, 2), pl.ds(start, turns * wide))
         return remote(
             zs.at[(slot, side) + part], z.at[(slot, 1 - side) + part],
-            d_send.at[slot, side, n], d_recv.at[slot, side, n], "down", side,
+            d_send.at[slot, side], d_recv.at[slot, side, group], "down", side,
         )
 
     def down_inner(slot, side):
         part = pl.ds(2, rows - 2)
         return remote(
             zs.at[slot, side, part], z.at[slot, 1 - side, part],
-            di_send.at[slot, side], di_recv.at[slot, side], "down", side,
+            d_send.at[slot, side], di_recv.at[slot, side], "down", side,
+        )
+
+    def down_sent(slot, side):
+        return remote(
+            zs.at[slot, side], z.at[slot, 1 - side],
+            d_send.at[slot, side], di_recv.at[slot, side], "down", side,
         )
 
     def east(slot, side, k, first=False):
@@ -113,7 +136,14 @@
         src = u_hbm.at[row - 1, here - 1] if first else ab.at[slot, row, here]
         return remote(
             src, ab.at[slot, row, there],
-            e_send.at[slot, side, k], e_recv.at[slot, side, k], "east", side,
+            e_send.at[slot, side], e_recv.at[slot, side], "east", side,
+        )
+
+    def east_both(slot, side):
+        both = pl.ds(1, 2)
+        return remote(
+            ab.at[slot, both, (1, cols)[side]], ab.at[slot, both, (cols + 1, 0)[side]],
+            e_send.at[slot, side], e_recv.at[slot, side], "east", side,
         )
 
     def east_inner(slot, side, first=False):
@@ -125,13 +155,15 @@
         )
         return remote(
             src, ab.at[slot, pl.ds(2, rows - 2), there],
-            ei_send.at[slot, side], ei_recv.at[slot, side], "east", side,
-        )
-
-    square = False
-    if relays:
-        relay_buf, h_recv, h_send, held, q_send, q_recv = hops
-    square = sizes["south"] == 4 and relays == {(2, 0): 0, (1, 1): 3}
+            e_send.at[slot, side], ei_recv.at[slot, side], "east", side,
+        )
+
+    def east_sent(slot, side):
+        own = pl.ds(1, rows)
+        return remote(
+            ab.at[slot, own, (1, cols)[side]], ab.at[slot, own, (cols + 1, 0)[side]],
+            e_send.at[slot, side], ei_recv.at[slot, side], "east", side,
+        )
 
     def by_place(table, other):
         value = jnp.int32(other)
@@ -154,7 +186,7 @@
         )
         return pltpu.make_async_remote_copy(
             src_ref=src, dst_ref=relay_buf.at[t, m],
-            send_sem=s_send.at[slot, side, n], recv_sem=h_recv.at[t, m],
+            send_sem=s_send.at[slot, side], recv_sem=h_recv.at[lax.rem(jnp.int32(t), 2), m],
             device_id={"south": jnp.maximum(relay_at[side], 0)}, device_id_type=MESH,
         )
 
@@ -166,7 +198,15 @@
         return pltpu.make_async_remote_copy(
             src_ref=relay_buf.at[t, m],
             dst_ref=ab.at[slot, there, pl.ds(n * wide + 1, wide)],
-            send_sem=h_send.at[t, m], recv_sem=s_recv.at[slot, served_side, n],
+            send_sem=h_send.at[slot], recv_sem=s_recv.at[slot, served_side, n],
+            device_id={"south": jnp.maximum(goal, 0)}, device_id_type=MESH,
+        )
+
+    def hops_sent(t):
+        goal = served + 2 * served_side - 1
+        return pltpu.make_async_remote_copy(
+            src_ref=relay_buf.at[t], dst_ref=relay_buf.at[t],
+            send_sem=h_send.at[lax.rem(jnp.int32(t), 2)], recv_sem=h_recv.at[0, 0],
             device_id={"south": jnp.maximum(goal, 0)}, device_id_type=MESH,
         )
 
@@ -174,6 +214,10 @@
         if relays:
             @pl.when(is_relay)
             def _():
+                @pl.when(jnp.logical_and(t >= 2, m == 0))
+                def _():
+                    hops_sent(t - 2).wait_send()
+
                 hop_in(t, 0, 0, 0, m).wait_recv()
                 hop_out(t, m).start()
 
@@ -283,10 +327,8 @@
             zs[0, 0, r, i] = ab[0, j + 1, i + 1, pl.ds(0, 1)]
             zs[0, 1, r, i] = ab[0, j + 1, i + 1, pl.ds(depth - 1, 1)]
 
-    @pl.loop(0, pieces)
-    def _(n):
-        each("start", sends, "down", lambda side: down(0, side, piece(n)))
-
+    for group in range(groups):
+        each("start", sends, "down", lambda side: down(0, side, group))
     each("start", sends, "down", lambda side: down_inner(0, side))
     loads[1].wait()
     loads[2].wait()
@@ -319,8 +361,9 @@
 
         @pl.when(step >= 1)
         def _():
-            each("wait_send", sends, "east", lambda side: east_inner(later, side))
-            each("wait_send", sends, "down", lambda side: down_inner(later, side))
+            each("wait_send", sends, "east", lambda side: east_sent(later, side))
+            each("wait_send", sends, "down", lambda side: down_sent(later, side))
+            each("wait_send", sends, "south", lambda side: south_sent(later, side))
 
         @pl.loop(1, rows - 1)
         def _(j):
@@ -333,26 +376,28 @@
             each("start", sends, "east", lambda side: east_inner(later, side))
             each("start", sends, "down", lambda side: down_inner(later, side))
 
-    def outer_edges(act, when, slot, n):
+    def edges_sent(slot, n):
         for side in (0, 1):
-            end = (0, pieces - 1)[side if when is sends else 1 - side]
-
-            @pl.when(jnp.logical_and(when("east", side), n == end))
+            @pl.when(jnp.logical_and(sends("east", side), n == (0, pieces - 1)[side]))
             def _():
                 for k in (0, 1):
-                    getattr(east(slot, side, k), act)()
+                    east(slot, side, k).start()
+
+    def edges_received(slot, n):
+        for side in (0, 1):
+            @pl.when(jnp.logical_and(receives("east", side), n == (pieces - 1, 0)[side]))
+            def _():
+                east_both(slot, side).wait_recv()
 
     def outer_piece(step, now, later, turn, final=False):
         n = piece(turn)
         each("wait_recv", receives, "south", lambda side: south(now, side, n))
-        each("wait_recv", receives, "down", lambda side: down(now, side, n))
-        outer_edges("wait_recv", receives, now, n)
-
-        @pl.when(step >= 1)
-        def _():
-            each("wait_send", sends, "south", lambda side: south(later, side, n))
-            each("wait_send", sends, "down", lambda side: down(later, side, n))
-            outer_edges("wait_send", sends, later, n)
+
+        @pl.when(lax.rem(turn, turns) == 0)
+        def _():
+            each("wait_recv", receives, "down", lambda side: down(now, side, turn // turns))
+
+        edges_received(now, n)
 
         @pl.loop(0, wide)
         def _(w):
@@ -363,8 +408,12 @@
         @pl.when(step < STEPS - 1)
         def _():
             send_south(step + 1, later, turn)
-            each("start", sends, "down", lambda side: down(later, side, n))
-            outer_edges("start", sends, later, n)
+
+            @pl.when(lax.rem(turn, turns) == turns - 1)
+            def _():
+                each("start", sends, "down", lambda side: down(later, side, turn // turns))
+
+            edges_sent(later, n)
 
     @pl.loop(0, STEPS - 1)
     def _(step):
@@ -389,7 +438,7 @@
     def carry(n):
         return remote(
             sbuf.at[pl.ds(n * wide, wide)], pin.at[pl.ds(n * wide, wide)],
-            p_send.at[n], p_recv.at[n], "south", 1,
+            p_send.at[0], p_recv.at[n], "south", 1,
         )
 
     first = jnp.logical_not(below["south"])
@@ -399,8 +448,14 @@
         part = pl.ds(n * wide, wide)
         return pltpu.make_async_remote_copy(
             src_ref=src.at[part], dst_ref=dst.at[part],
-            send_sem=q_send.at[way, n], recv_sem=q_recv.at[kind, n],
+            send_sem=q_send.at[way], recv_sem=q_recv.at[kind, n],
             device_id={"south": goal}, device_id_type=MESH,
+        )
+
+    def totals_sent(way):
+        return pltpu.make_async_remote_copy(
+            src_ref=sbuf, dst_ref=pin, send_sem=q_send.at[way], recv_sem=q_recv.at[0, 0],
+            device_id={"south": lax.rem(spot + 1, 4)}, device_id_type=MESH,
         )
 
     def beside(n):
@@ -490,6 +545,17 @@
         def _(turn):
             middle_total(turn)
 
+    if relays:
+        @pl.when(is_relay)
+        def _():
+            for t in range(max(STEPS - 2, 0), STEPS):
+                hops_sent(t).wait_send()
+
+    each("wait_send", sends, "east", lambda side: east_sent(now, side))
+    each("wait_send", sends, "down", lambda side: down_sent(now, side))
+    each("wait_send", sends, "south", lambda side: south_sent(now, side))
+
+    if square:
         @pl.when(spot == 1)
         def _():
             @pl.loop(0, pieces)
@@ -538,59 +604,43 @@
                 def _():
                     carry(n).start()
 
-    if relays:
-        @pl.when(is_relay)
-        def _():
-            for t in range(STEPS):
-                for m in range(pieces // 2):
-                    hop_out(t, m).wait_send()
-
-    each("wait_send", sends, "east", lambda side: east_inner(now, side))
-    each("wait_send", sends, "down", lambda side: down_inner(now, side))
-    for k in (0, 1):
-        each("wait_send", sends, "east", lambda side: east(now, side, k))
-
-    @pl.loop(0, pieces)
-    def _(n):
-        each("wait_send", sends, "south", lambda side: south(now, side, n))
-        each("wait_send", sends, "down", lambda side: down(now, side, n))
-
-        if square:
-            @pl.when(lax.rem(spot, 2) == 0)
-            def _():
-                beside(n).wait_send()
-
-            @pl.when(spot != 2)
-            def _():
-                across(n).wait_send()
-        else:
-            @pl.when(above["south"])
-            def _():
-                carry(n).wait_send()
-
-
-def writer(part, end, before, total_hbm, end_hbm, total, t_sem, e_sem):
+    if square:
+        @pl.when(lax.rem(spot, 2) == 0)
+        def _():
+            totals_sent(0).wait_send()
+
+        @pl.when(spot != 2)
+        def _():
+            totals_sent(1).wait_send()
+    else:
+        @pl.when(above["south"])
+        def _():
+            remote(sbuf, pin, p_send.at[0], p_recv.at[0], "south", 1).wait_send()
+
+
+def writer(part, end, before, total_hbm, end_hbm, total, sem):
     rows, cols = part.shape[:2]
-    ends = [pltpu.make_async_copy(end.at[j], end_hbm.at[j], e_sem.at[j]) for j in range(rows)]
-    totals = [
-        pltpu.make_async_copy(total.at[j], total_hbm.at[j], t_sem.at[j]) for j in range(rows)
-    ]
-    for copy in ends:
-        copy.start()
+    for j in range(rows):
+        pltpu.make_async_copy(end.at[j], end_hbm.at[j], sem.at[0]).start()
     for j in range(rows):
         @pl.loop(0, cols)
         def _(i):
             total[j, i] = part[j, i] + before[i]
 
-        totals[j].start()
-    for copy in ends + totals:
-        copy.wait()
+        pltpu.make_async_copy(total.at[j], total_hbm.at[j], sem.at[1]).start()
+    pltpu.make_async_copy(end, end_hbm, sem.at[0]).wait()
+    pltpu.make_async_copy(total, total_hbm, sem.at[1]).wait()
+
+
+def is_square(sizes, relays):
+    return sizes["south"] == 4 and relays == {(2, 0): 0, (1, 1): 3}
 
 
 def shards(sizes, relays, field_now, earlier, speed_square):
     rows, cols, depth, lanes = field_now.shape
     pieces = min(PIECES, cols)
     relays = relays if pieces % 2 == 0 else {}
+    groups = 2 if pieces % 2 == 0 else 1
     edge = (2, 2, rows, cols, 1, lanes)
     dma = pltpu.SemaphoreType.DMA
     anywhere = pl.BlockSpec(memory_space=pltpu.HBM)
@@ -610,17 +660,14 @@
             pltpu.VMEM(edge, jnp.float32),
             pltpu.VMEM((cols, depth, lanes), jnp.float32),
             pltpu.VMEM((cols, depth, lanes), jnp.float32),
-            dma((2, 2, pieces)), dma((2, 2, pieces)),
-            dma((2, 2, pieces)), dma((2, 2, pieces)),
-            dma((2, 2, 2)), dma((2, 2, 2)),
-            dma((2, 2)), dma((2, 2)), dma((2, 2)), dma((2, 2)),
-            dma((pieces,)), dma((pieces,)), dma((3,)),
+            dma((2, 2)), dma((2, 2, pieces)), dma((2, 2)), dma((2, 2, groups)),
+            dma((2, 2)), dma((2, 2)), dma((2, 2)), dma((2, 2)), dma((3,)),
         ] + ([
             pltpu.VMEM((STEPS, pieces // 2, cols // pieces, depth, lanes), jnp.float32),
-            dma((STEPS, pieces // 2)), dma((STEPS, pieces // 2)),
-            pltpu.VMEM((cols, depth, lanes), jnp.float32),
-            dma((2, pieces)), dma((2, pieces)),
-        ] if relays else []),
+            dma((2, pieces // 2)), dma((2,)),
+        ] if relays else []) + ([
+            pltpu.VMEM((cols, depth, lanes), jnp.float32), dma((2,)), dma((2, pieces)),
+        ] if is_square(sizes, relays) else [dma((1,)), dma((pieces,))]),
         compiler_params=pltpu.CompilerParams(
             collective_id=0, has_side_effects=True, vmem_limit_bytes=VMEM_LIMIT
         ),
@@ -631,7 +678,7 @@
         out_shape=(jax.ShapeDtypeStruct(field_now.shape, jnp.float32),) * 2,
         in_specs=[inside] * 3,
         out_specs=(anywhere,) * 2,
-        scratch_shapes=[pltpu.VMEM(field_now.shape, jnp.float32), dma((rows,)), dma((rows,))],
+        scratch_shapes=[pltpu.VMEM(field_now.shape, jnp.float32), dma((2,))],
         compiler_params=pltpu.CompilerParams(vmem_limit_bytes=WRITER_LIMIT),
         name="write",
     )(part, end, before)

time: 170 us -> 169 us (level)
  no operation moved by 1% of the time
where the time goes in v3:
time: 169 us; the launch traced here: 168 us
  Pallas kernels  168 us (99%)
    pallas_call x1, Pallas kernels, shards(): pl.pallas_call(functools.partial(kernel, sizes, relays), out_shape=(pltpu...  162 us
    pallas_call x1, Pallas kernels, shards(): pl.pallas_call(writer, out_shape=(jax.ShapeDtypeStruct(field_now.shape, j...  5.84 us

profile of v3, /device:TPU:4, one launch (start us, length us, event | category | flops | bytes accessed | tf_op | source)
XLA Modules:
  0.0 168.4 jit_solution(6175370100499586339)
XLA Ops:
  0.6 161.9 %wave.1 = (f32[8,16,128,128]{3,2,1,0:T(8,128)S(1)}, f32[8,16,128,128]{3,2,1,0:T(8,128)S(1)}, f32[16,128,128]{2,1,0:T(8,128)S(1)}) custom-call(f32[8,16,128,128]{3,2,1,0:T(8,128)} %u_hbm.1, f32[8,16,128,128]{3,2,1,0:T(8,128)} %e_hbm.1, f32[8,16,128,128]{3,2,1,0:T(8,128)} %c_hbm.1), custom_call_target="tpu_custom_call" | custom-call | tf_op jit(solution)/shard_map/wave/pallas_call | solution.py:648
  162.6 5.8 %write.1 = (f32[8,16,128,128]{3,2,1,0:T(8,128)}, f32[8,16,128,128]{3,2,1,0:T(8,128)}) custom-call(f32[8,16,128,128]{3,2,1,0:T(8,128)S(1)} %get-tuple-element.5.part, f32[8,16,128,128]{3,2,1,0:T(8,128)S(1)} %get-tuple-element.6.end, f32[16,128,128]{2,1,0:T(8,128)S(1)} %get-tuple-element.7.before), custom_call_target="tpu_custom_call" | custom-call | tf_op jit(solution)/shard_map/write/pallas_call | solution.py:676

commit v4 on v3

--- a/solution.py
+++ b/solution.py
@@ -9,7 +9,7 @@
 from jax.sharding import PartitionSpec as P
 
 STEPS = 4
-PIECES = 8
+PIECES = 4
 VMEM_LIMIT = 42 * 1024 * 1024
 WRITER_LIMIT = 12 * 1024 * 1024
 VIA = 1
@@ -452,9 +452,13 @@
             device_id={"south": goal}, device_id_type=MESH,
         )
 
-    def totals_sent(way):
+    early = pieces // 4
+
+    def totals_sent(way, count=pieces):
+        part = pl.ds(0, count * wide)
         return pltpu.make_async_remote_copy(
-            src_ref=sbuf, dst_ref=pin, send_sem=q_send.at[way], recv_sem=q_recv.at[0, 0],
+            src_ref=sbuf.at[part], dst_ref=pin.at[part],
+            send_sem=q_send.at[way], recv_sem=q_recv.at[0, 0],
             device_id={"south": lax.rem(spot + 1, 4)}, device_id_type=MESH,
         )
 
@@ -466,6 +470,9 @@
 
     def upward(n):
         return total_copy(n, sbuf, held, 1, 1, 3)
+
+    def direct(n):
+        return total_copy(n, sbuf, held, 0, 1, 2)
 
     def onward(n):
         return total_copy(n, held, held, 1, 1, 2)
@@ -487,7 +494,10 @@
         @pl.when(spot == 3)
         def _():
             upward(n).wait_recv()
-            onward(n).start()
+
+            @pl.when(turn >= early)
+            def _():
+                onward(n).start()
 
     @pl.loop(0, pieces)
     def _(turn):
@@ -519,6 +529,10 @@
             def _():
                 upward(n).start()
 
+                @pl.when(turn < early)
+                def _():
+                    direct(n).start()
+
             @pl.when(turn >= 2)
             def _():
                 middle_total(turn - 2)
@@ -609,9 +623,18 @@
         def _():
             totals_sent(0).wait_send()
 
-        @pl.when(spot != 2)
+        @pl.when(spot < 2)
         def _():
             totals_sent(1).wait_send()
+
+        if early:
+            @pl.when(spot == 1)
+            def _():
+                totals_sent(0, early).wait_send()
+
+        @pl.when(spot == 3)
+        def _():
+            totals_sent(1, pieces - early).wait_send()
     else:
         @pl.when(above["south"])
         def _():

time: 169 us -> 168 us (level)
  Pallas kernels: 168 us -> 166 us
    pallas_call x1, Pallas kernels: 162 us -> 160 us  [shards(): pl.pallas_call(functools.partial(kernel, sizes, relays), out_shape=(pltpu...]
where the time goes in v4:
time: 168 us; the launch traced here: 166 us
  Pallas kernels  166 us (99%)
    pallas_call x1, Pallas kernels, shards(): pl.pallas_call(functools.partial(kernel, sizes, relays), out_shape=(pltpu...  160 us
    pallas_call x1, Pallas kernels, shards(): pl.pallas_call(writer, out_shape=(jax.ShapeDtypeStruct(field_now.shape, j...  5.84 us

profile of v4, /device:TPU:4, one launch (start us, length us, event | category | flops | bytes accessed | tf_op | source)
XLA Modules:
  0.0 166.2 jit_solution(14953316631858746529)
XLA Ops:
  0.6 159.7 %wave.1 = (f32[8,16,128,128]{3,2,1,0:T(8,128)S(1)}, f32[8,16,128,128]{3,2,1,0:T(8,128)S(1)}, f32[16,128,128]{2,1,0:T(8,128)S(1)}) custom-call(f32[8,16,128,128]{3,2,1,0:T(8,128)} %u_hbm.1, f32[8,16,128,128]{3,2,1,0:T(8,128)} %e_hbm.1, f32[8,16,128,128]{3,2,1,0:T(8,128)} %c_hbm.1), custom_call_target="tpu_custom_call" | custom-call | tf_op jit(solution)/shard_map/wave/pallas_call | solution.py:671
  160.4 5.8 %write.1 = (f32[8,16,128,128]{3,2,1,0:T(8,128)}, f32[8,16,128,128]{3,2,1,0:T(8,128)}) custom-call(f32[8,16,128,128]{3,2,1,0:T(8,128)S(1)} %get-tuple-element.5.part, f32[8,16,128,128]{3,2,1,0:T(8,128)S(1)} %get-tuple-element.6.end, f32[16,128,128]{2,1,0:T(8,128)S(1)} %get-tuple-element.7.before), custom_call_target="tpu_custom_call" | custom-call | tf_op jit(solution)/shard_map/write/pallas_call | solution.py:699

commit v5 on v4

--- a/solution.py
+++ b/solution.py
@@ -48,13 +48,11 @@
 def kernel(
     sizes, relays, u_hbm, e_hbm, c_hbm, c, end, before,
     ab, z, zs, pin, sbuf,
-    s_send, s_recv, d_send, d_recv, e_send, e_recv, ei_recv, di_recv, load_sem, *extra,
+    s_send, s_recv, d_send, d_recv, e_send, e_recv, di_recv, load_sem, *extra,
 ):
     rows, cols, depth, lanes = u_hbm.shape
     pieces = min(PIECES, cols)
     wide = cols // pieces
-    groups = d_recv.shape[2]
-    turns = pieces // groups
     square = is_square(sizes, relays)
     extra = list(extra)
     if relays:
@@ -108,12 +106,11 @@
             row, row, s_send.at[slot, side], s_recv.at[slot, side, 0], "south", side
         )
 
-    def down(slot, side, group):
-        start = jnp.where(odd, group, groups - 1 - group) * turns * wide
-        part = (pl.ds(0, 2), pl.ds(start, turns * wide))
+    def down(slot, side):
+        part = pl.ds(0, 2)
         return remote(
-            zs.at[(slot, side) + part], z.at[(slot, 1 - side) + part],
-            d_send.at[slot, side], d_recv.at[slot, side, group], "down", side,
+            zs.at[slot, side, part], z.at[slot, 1 - side, part],
+            d_send.at[slot, side], d_recv.at[slot, side], "down", side,
         )
 
     def down_inner(slot, side):
@@ -129,40 +126,14 @@
             d_send.at[slot, side], di_recv.at[slot, side], "down", side,
         )
 
-    def east(slot, side, k, first=False):
+    def east(slot, side, first=False):
         here = (1, cols)[side]
         there = (cols + 1, 0)[side]
-        row = (1, rows)[k]
-        src = u_hbm.at[row - 1, here - 1] if first else ab.at[slot, row, here]
+        own = pl.ds(1, rows)
+        src = u_hbm.at[pl.ds(0, rows), here - 1] if first else ab.at[slot, own, here]
         return remote(
-            src, ab.at[slot, row, there],
+            src, ab.at[slot, own, there],
             e_send.at[slot, side], e_recv.at[slot, side], "east", side,
-        )
-
-    def east_both(slot, side):
-        both = pl.ds(1, 2)
-        return remote(
-            ab.at[slot, both, (1, cols)[side]], ab.at[slot, both, (cols + 1, 0)[side]],
-            e_send.at[slot, side], e_recv.at[slot, side], "east", side,
-        )
-
-    def east_inner(slot, side, first=False):
-        here = (1, cols)[side]
-        there = (cols + 1, 0)[side]
-        src = (
-            u_hbm.at[pl.ds(1, rows - 2), here - 1]
-            if first else ab.at[slot, pl.ds(2, rows - 2), here]
-        )
-        return remote(
-            src, ab.at[slot, pl.ds(2, rows - 2), there],
-            e_send.at[slot, side], ei_recv.at[slot, side], "east", side,
-        )
-
-    def east_sent(slot, side):
-        own = pl.ds(1, rows)
-        return remote(
-            ab.at[slot, own, (1, cols)[side]], ab.at[slot, own, (cols + 1, 0)[side]],
-            e_send.at[slot, side], ei_recv.at[slot, side], "east", side,
         )
 
     def by_place(table, other):
@@ -288,9 +259,7 @@
     def _(n):
         send_south(0, 0, n, True)
 
-    for k in (0, 1):
-        each("start", sends, "east", lambda side: east(0, side, k, True))
-    each("start", sends, "east", lambda side: east_inner(0, side, True))
+    each("start", sends, "east", lambda side: east(0, side, True))
     loads[1].start()
     loads[2].start()
 
@@ -327,8 +296,7 @@
             zs[0, 0, r, i] = ab[0, j + 1, i + 1, pl.ds(0, 1)]
             zs[0, 1, r, i] = ab[0, j + 1, i + 1, pl.ds(depth - 1, 1)]
 
-    for group in range(groups):
-        each("start", sends, "down", lambda side: down(0, side, group))
+    each("start", sends, "down", lambda side: down(0, side))
     each("start", sends, "down", lambda side: down_inner(0, side))
     loads[1].wait()
     loads[2].wait()
@@ -356,12 +324,12 @@
         zs[later, 1, r, i] = new[depth - 1:]
 
     def inner(step, now, later, final=False):
-        each("wait_recv", receives, "east", lambda side: east_inner(now, side))
+        each("wait_recv", receives, "east", lambda side: east(now, side))
         each("wait_recv", receives, "down", lambda side: down_inner(now, side))
 
         @pl.when(step >= 1)
         def _():
-            each("wait_send", sends, "east", lambda side: east_sent(later, side))
+            each("wait_send", sends, "east", lambda side: east(later, side))
             each("wait_send", sends, "down", lambda side: down_sent(later, side))
             each("wait_send", sends, "south", lambda side: south_sent(later, side))
 
@@ -373,31 +341,21 @@
 
         @pl.when(step < STEPS - 1)
         def _():
-            each("start", sends, "east", lambda side: east_inner(later, side))
             each("start", sends, "down", lambda side: down_inner(later, side))
 
     def edges_sent(slot, n):
         for side in (0, 1):
             @pl.when(jnp.logical_and(sends("east", side), n == (0, pieces - 1)[side]))
             def _():
-                for k in (0, 1):
-                    east(slot, side, k).start()
-
-    def edges_received(slot, n):
-        for side in (0, 1):
-            @pl.when(jnp.logical_and(receives("east", side), n == (pieces - 1, 0)[side]))
-            def _():
-                east_both(slot, side).wait_recv()
+                east(slot, side).start()
 
     def outer_piece(step, now, later, turn, final=False):
         n = piece(turn)
         each("wait_recv", receives, "south", lambda side: south(now, side, n))
 
-        @pl.when(lax.rem(turn, turns) == 0)
-        def _():
-            each("wait_recv", receives, "down", lambda side: down(now, side, turn // turns))
-
-        edges_received(now, n)
+        @pl.when(turn == 0)
+        def _():
+            each("wait_recv", receives, "down", lambda side: down(now, side))
 
         @pl.loop(0, wide)
         def _(w):
@@ -409,9 +367,9 @@
         def _():
             send_south(step + 1, later, turn)
 
-            @pl.when(lax.rem(turn, turns) == turns - 1)
-            def _():
-                each("start", sends, "down", lambda side: down(later, side, turn // turns))
+            @pl.when(turn == pieces - 1)
+            def _():
+                each("start", sends, "down", lambda side: down(later, side))
 
             edges_sent(later, n)
 
@@ -565,7 +523,7 @@
             for t in range(max(STEPS - 2, 0), STEPS):
                 hops_sent(t).wait_send()
 
-    each("wait_send", sends, "east", lambda side: east_sent(now, side))
+    each("wait_send", sends, "east", lambda side: east(now, side))
     each("wait_send", sends, "down", lambda side: down_sent(now, side))
     each("wait_send", sends, "south", lambda side: south_sent(now, side))
 
@@ -663,7 +621,6 @@
     rows, cols, depth, lanes = field_now.shape
     pieces = min(PIECES, cols)
     relays = relays if pieces % 2 == 0 else {}
-    groups = 2 if pieces % 2 == 0 else 1
     edge = (2, 2, rows, cols, 1, lanes)
     dma = pltpu.SemaphoreType.DMA
     anywhere = pl.BlockSpec(memory_space=pltpu.HBM)
@@ -683,8 +640,8 @@
             pltpu.VMEM(edge, jnp.float32),
             pltpu.VMEM((cols, depth, lanes), jnp.float32),
             pltpu.VMEM((cols, depth, lanes), jnp.float32),
-            dma((2, 2)), dma((2, 2, pieces)), dma((2, 2)), dma((2, 2, groups)),
-            dma((2, 2)), dma((2, 2)), dma((2, 2)), dma((2, 2)), dma((3,)),
+            dma((2, 2)), dma((2, 2, pieces)), dma((2, 2)), dma((2, 2)),
+            dma((2, 2)), dma((2, 2)), dma((2, 2)), dma((3,)),
         ] + ([
             pltpu.VMEM((STEPS, pieces // 2, cols // pieces, depth, lanes), jnp.float32),
             dma((2, pieces // 2)), dma((2,)),

time: 168 us -> 168 us (level)
  no operation moved by 1% of the time
where the time goes in v5:
time: 168 us; the launch traced here: 166 us
  Pallas kernels  165 us (98%)
    pallas_call x1, Pallas kernels, shards(): pl.pallas_call(functools.partial(kernel, sizes, relays), out_shape=(pltpu...  160 us
    pallas_call x1, Pallas kernels, shards(): pl.pallas_call(writer, out_shape=(jax.ShapeDtypeStruct(field_now.shape, j...  5.84 us

profile of v5, /device:TPU:4, one launch (start us, length us, event | category | flops | bytes accessed | tf_op | source)
XLA Modules:
  0.0 166.1 jit_solution(15007234112000279595)
XLA Ops:
  0.6 159.6 %wave.1 = (f32[8,16,128,128]{3,2,1,0:T(8,128)S(1)}, f32[8,16,128,128]{3,2,1,0:T(8,128)S(1)}, f32[16,128,128]{2,1,0:T(8,128)S(1)}) custom-call(f32[8,16,128,128]{3,2,1,0:T(8,128)} %u_hbm.1, f32[8,16,128,128]{3,2,1,0:T(8,128)} %e_hbm.1, f32[8,16,128,128]{3,2,1,0:T(8,128)} %c_hbm.1), custom_call_target="tpu_custom_call" | custom-call | tf_op jit(solution)/shard_map/wave/pallas_call | solution.py:628
  160.3 5.8 %write.1 = (f32[8,16,128,128]{3,2,1,0:T(8,128)}, f32[8,16,128,128]{3,2,1,0:T(8,128)}) custom-call(f32[8,16,128,128]{3,2,1,0:T(8,128)S(1)} %get-tuple-element.5.part, f32[8,16,128,128]{3,2,1,0:T(8,128)S(1)} %get-tuple-element.6.end, f32[16,128,128]{2,1,0:T(8,128)S(1)} %get-tuple-element.7.before), custom_call_target="tpu_custom_call" | custom-call | tf_op jit(solution)/shard_map/write/pallas_call | solution.py:656
